TPU v7x, 32 devices: a whole 2x2x4 slice. The times are simulated.
32 devices in a mesh: groups: 2 (over y), rows: 4 (over z), keys: 2 (over x), heads: 2 (over core).
Axes of the slice: x: 2, y: 2, z: 4, core: 2. Of those that a mesh axis runs over, the one named last changes fastest.
Arguments:
- pair: bfloat16 [1024, 512, 128], P(('groups', 'rows'), 'keys'), parts along dimension 0, may hold values from -6 to 6
- seq_length: int32 [2], P('groups'), parts along dimension 0, may hold values from 257 to 512
- tile_counts: int32 [1024, 4], P(('groups', 'rows')), parts along dimension 0, may hold values from 0 to 128, as said below
- ln_gain: float32 [128], replicated, may hold values from 0.5 to 1.5
- w_query: bfloat16 [128, 128], P(None, 'heads'), may hold values from -8 to 8
- w_key: bfloat16 [128, 128], P(None, 'heads'), may hold values from -0.5 to 0.5
- w_value: bfloat16 [128, 128], P(None, 'heads'), may hold values from -0.5 to 0.5
- w_gate: bfloat16 [128, 128], P(None, 'heads'), may hold values from -0.5 to 0.5
- w_bias: bfloat16 [128, 4], P(None, 'heads'), may hold values from -1.5 to 1.5
- w_out: bfloat16 [128, 128], replicated, may hold values from -2 to 2
Outputs:
- update: bfloat16 [1024, 512, 128], P(('groups', 'rows'), ('keys', 'heads')), parts along dimension 0
There are 2 independent parts, one for each index of `groups`. A program takes and returns all parts, laid end to end along the dimension named above; an argument that names none is the same for every part. Nothing has to cross between parts.
Inputs may be any that keep to these rules, and one draw needn't show every extreme that they name: `tile_counts`: for each row and each tile of 128 keys, how many of the tile's leading keys are valid; some rows have no valid key at all.
All inputs are finite; a program needn't handle non-finite values.
Results may differ from a plain program's by a relative error of at most 0.03.
The roundings to bfloat16 on the way count: a program that leaves them out, or rounds other values in their place, can miss the bound.
Values may be sent and summed in bfloat16 or wider, within the bound.
A program may use at most 192 MiB of HBM per device.

v0:
```python
import jax
import jax.numpy as jnp
from jax import lax
from jax.sharding import PartitionSpec as P

HEAD_DIM = 32
TILE = 128
norm_epsilon = 1e-05
masked_score = -1e30


def layer_norm(values, gain):
    center = values - jnp.mean(values, axis=-1, keepdims=True)
    spread = jnp.mean(center * center, axis=-1, keepdims=True)
    return center * lax.rsqrt(spread + norm_epsilon) * gain


def finish(row_sum, weighted):
    denom = jnp.maximum(row_sum, 1.0)
    result = weighted / denom[..., None]
    rows_dev, heads_dev, cols_dev, depth = result.shape
    result = jnp.transpose(result, (0, 2, 1, 3)).reshape(rows_dev, cols_dev, heads_dev * depth)
    return result.astype(jnp.bfloat16)


def per_device(
    pair, seq_length, tile_counts, ln_gain, w_query, w_key, w_value, w_gate, w_bias, w_out
):
    rows_dev, cols_dev, channels = pair.shape
    key_groups = lax.axis_size("keys")
    length_all = cols_dev * key_groups
    heads_dev = w_bias.shape[1]
    width_dev = heads_dev * HEAD_DIM
    normed = layer_norm(pair.astype(jnp.float32), ln_gain).astype(jnp.bfloat16)
    flat = normed.reshape(rows_dev * cols_dev, channels)
    queries = (
        (jnp.dot(flat, w_query, preferred_element_type=jnp.float32) * HEAD_DIM ** (-0.5))
        .astype(jnp.bfloat16)
        .reshape(rows_dev, cols_dev, heads_dev, HEAD_DIM)
    )
    keys_local = (
        jnp.dot(flat, w_key, preferred_element_type=jnp.float32)
        .astype(jnp.bfloat16)
        .reshape(rows_dev, cols_dev, heads_dev, HEAD_DIM)
    )
    values_local = (
        jnp.dot(flat, w_value, preferred_element_type=jnp.float32)
        .astype(jnp.bfloat16)
        .reshape(rows_dev, cols_dev, heads_dev, HEAD_DIM)
    )
    gate_act = jax.nn.sigmoid(jnp.dot(flat, w_gate, preferred_element_type=jnp.float32)).reshape(
        rows_dev, cols_dev, width_dev
    )
    bias_local = jnp.einsum("rkc,ch->hrk", normed, w_bias, preferred_element_type=jnp.float32)
    bias_rows = lax.all_gather(bias_local.astype(jnp.bfloat16), "rows", axis=1, tiled=True).astype(
        bias_local.dtype
    )
    positions = jnp.arange(length_all, dtype=jnp.int32)
    allowed = (positions[None, :] < seq_length[0]) & (
        (positions % TILE)[None, :] < jnp.repeat(tile_counts, TILE, axis=1)
    )
    bias_turn = lax.all_to_all(
        bias_rows.astype(jnp.bfloat16), "keys", split_axis=1, concat_axis=2, tiled=True
    ).astype(bias_rows.dtype)
    initial = (
        jnp.full((rows_dev, heads_dev, cols_dev), masked_score, jnp.float32),
        jnp.zeros((rows_dev, heads_dev, cols_dev), jnp.float32),
        jnp.zeros((rows_dev, heads_dev, cols_dev, HEAD_DIM), jnp.float32),
    )
    piece_keys = lax.all_gather(keys_local, "keys", axis=1, tiled=True)
    piece_values = lax.all_gather(values_local, "keys", axis=1, tiled=True)

    def one_tile(tile_index, state):
        row_max, row_sum, weighted = state
        offset = tile_index * TILE
        key_tile = lax.dynamic_slice_in_dim(piece_keys, offset, TILE, 1)
        value_tile = lax.dynamic_slice_in_dim(piece_values, offset, TILE, 1)
        tile_bias = lax.dynamic_slice_in_dim(bias_turn, offset, TILE, 2)
        shown = lax.dynamic_slice_in_dim(allowed, offset, TILE, 1)[:, None, None, :]
        scores = (
            jnp.einsum("rjhd,rkhd->rhjk", queries, key_tile, preferred_element_type=jnp.float32)
            + tile_bias[None]
        )
        scores = jnp.where(shown, scores, masked_score)
        new_max = jnp.maximum(row_max, jnp.max(scores, axis=-1))
        weights = jnp.where(shown, jnp.exp(scores - new_max[..., None]), 0.0)
        rescale = jnp.exp(row_max - new_max)
        row_sum = row_sum * rescale + jnp.sum(weights, axis=-1)
        weighted = weighted * rescale[..., None] + jnp.einsum(
            "rhjk,rkhd->rhjd",
            weights.astype(jnp.bfloat16),
            value_tile,
            preferred_element_type=jnp.float32,
        )
        return (new_max, row_sum, weighted)

    row_max, row_sum, weighted = lax.fori_loop(0, piece_keys.shape[1] // TILE, one_tile, initial)
    attended = finish(row_sum, weighted)
    attended = lax.optimization_barrier(attended).astype(jnp.float32)
    gated = (gate_act * attended).astype(jnp.bfloat16)
    head_rank = lax.axis_index("heads")
    w_rows = lax.dynamic_slice_in_dim(w_out, head_rank * width_dev, width_dev, 0)
    partial_out = jnp.einsum("rkc,cd->rkd", gated, w_rows, preferred_element_type=jnp.float32)
    return lax.psum_scatter(
        partial_out.astype(jnp.bfloat16), "heads", scatter_dimension=1, tiled=True
    )


def solution(mesh):
    in_specs = (
        P(("groups", "rows"), "keys", None),
        P("groups"),
        P(("groups", "rows"), None),
        P(),
        P(None, "heads"),
        P(None, "heads"),
        P(None, "heads"),
        P(None, "heads"),
        P(None, "heads"),
        P(),
    )
    out_specs = P(("groups", "rows"), ("keys", "heads"), None)
    return jax.shard_map(
        per_device, mesh=mesh, in_specs=in_specs, out_specs=out_specs, check_vma=False
    )
```

profile of v0, /device:TPU:0, one launch (start us, length us, event | category | flops | bytes accessed | tf_op | source)
XLA Modules:
  0.0 505.1 jit_solution(12324241964965826432)
XLA Ops:
  6.5 5.8 %convert_reduce_fusion = f32[128,256]{1,0:T(8,128)S(1)} fusion(bf16[128,256,128]{2,1,0:T(8,128)(2,1)} %param.12), kind=kLoop, calls=%fused_computation.33 | loop fusion | flops 8355840 | bytes 8519680 | tf_op jit(solution)/shard_map/reduce_sum | solution.py:13
  12.4 10.9 %fusion.25 = f32[128,256]{1,0:T(8,128)S(1)} fusion(bf16[128,256,128]{2,1,0:T(8,128)(2,1)} %param.12, f32[128,256]{1,0:T(8,128)S(1)} %broadcast_multiply_fusion), kind=kLoop, calls=%fused_computation.36 | loop fusion | flops 16744448 | bytes 8650752 | tf_op jit(solution)/shard_map/reduce_sum | solution.py:14
  23.3 9.9 %fusion.27 = bf16[128,256,128]{2,1,0:T(8,128)(2,1)S(1)} fusion(bf16[128,256,128]{2,1,0:T(8,128)(2,1)S(1)} %bitcast.83, f32[128]{0:T(128)S(1)} %copy-done.9, f32[128,256]{1,0:T(8,128)S(1)} %add_rsqrt_fusion, f32[128,256]{1,0:T(8,128)S(1)} %broadcast_multiply_fusion), kind=kLoop, calls=%fused_computation.38 | loop fusion | flops 20971520 | bytes 17039872 | tf_op jit(solution)/shard_map/convert_element_type | solution.py:34
  40.6 4.4 copy.20
  45.3 6.4 %convolution_convert_fusion = bf16[32768,64]{0,1:T(8,128)(2,1)S(1)} fusion(bf16[32768,128]{1,0:T(8,128)(2,1)} %bitcast.79, bf16[128,64]{0,1:T(8,128)(2,1)S(1)} %copy-done.6), kind=kOutput, calls=%fused_computation.29 | convolution fusion | flops 538968064 | bytes 12599296 | tf_op jit(solution)/shard_map/dot_general | solution.py:47
  52.9 4.6 copy.22
  57.5 6.8 %fusion.30 = bf16[2,128,256]{2,0,1:T(2,128)(2,1)S(1)} fusion(bf16[128,256,128]{2,1,0:T(8,128)(2,1)} %copy-done.1, bf16[128,2]{0,1:T(2,128)(2,1)S(1)} %copy-done.10), kind=kOutput, calls=%fused_computation.44 | convolution fusion | flops 16842752 | bytes 8520192 | tf_op jit(solution)/shard_map/rkc,ch->hrk/dot_general | solution.py:54
  64.3 17.8 %all_gather.10 = bf16[2,512,256]{2,0,1:T(2,128)(2,1)} all-gather(bf16[2,128,256]{2,0,1:T(2,128)(2,1)S(1)} %fusion.30), channel_id=1, replica_groups=mesh['groups'=2,'rows'=4,'keys'=2,'heads'=2] {'rows'}, dimensions={1}, use_global_device_ids=true | all-gather | bytes 655360 | tf_op jit(solution)/shard_map/all_gather | solution.py:55
  82.1 3.5 all-to-all-start
  86.5 8.3 %fusion.21 = bf16[32768,64]{0,1:T(8,128)(2,1)} fusion(bf16[32768,128]{1,0:T(8,128)(2,1)} %bitcast.80, bf16[128,64]{0,1:T(8,128)(2,1)S(1)} %copy-done.7), kind=kOutput, calls=%fused_computation.28 | convolution fusion | flops 541065216 | bytes 12599296 | tf_op jit(solution)/shard_map/dot_general | solution.py:37
  94.9 9.7 %fusion.22 = f32[32768,64]{0,1:T(8,128)} fusion(bf16[32768,128]{1,0:T(8,128)(2,1)} %bitcast.81, bf16[128,64]{0,1:T(8,128)(2,1)S(1)} %copy-done.11), kind=kOutput, calls=%fused_computation.31 | convolution fusion | flops 543162368 | bytes 16793600 | tf_op jit(solution)/shard_map/dot_general | solution.py:51
  104.6 3.3 copy.29
  107.8 4.4 copy.23
  113.8 43.7 %all-gather.3.cloned.1.call-done = bf16[128,512,2,32]{1,3,2,0:T(8,128)(2,1)} async-done(((bf16[128,256,2,32]{1,3,2,0:T(8,128)(2,1)}), bf16[128,512,2,32]{1,3,2,0:T(8,128)(2,1)}) %all-gather.3.cloned.1.call-update) | async-done | bytes 8388624 | tf_op jit(solution)/shard_map/all_gather | solution.py:70
  157.5 105.5 %all-gather.5.cloned.1.call-done = bf16[128,512,2,32]{1,3,2,0:T(8,128)(2,1)} async-done(((bf16[128,256,2,32]{1,3,2,0:T(8,128)(2,1)}), bf16[128,512,2,32]{1,3,2,0:T(8,128)(2,1)}) %all-gather.5.cloned.1.call-update) | async-done | bytes 8388624 | tf_op jit(solution)/shard_map/all_gather | solution.py:71
  263.1 208.6 %while.18 = (s32[]{:T(128)}, f32[128,2,256]{2,1,0:T(2,128)S(1)}, f32[128,2,256]{2,1,0:T(2,128)S(1)}, f32[128,2,256,32]{2,3,1,0:T(8,128)}, pred[128,512]{1,0:T(8,...) while((s32[]{:T(128)}, f32[128,2,256]{2,1,0:T(2,128)S(1)}, ...), condition=%wide.region_5.6_spmd.clone, body=%wide.region_2.5_spmd.clone.sunk | while | flops 1189412864 | bytes 198525168 | solution.py:97
  263.1 16.2 %fusion.60 = (f32[128,2,256]{2,1,0:T(2,128)S(1)}, f32[128,2,128,256]{3,2,1,0:T(8,128)}) fusion(f32[2,256,128]{1,2,0:T(8,128)S(1)} %constant_dynamic-slice_fusion.4, pred[128,128]{1,0:T(8,128)(4,1)S(1)} %constant_dynamic-slice_fusion.5, bf16[128,256,2,32]{1,3,2,0:T(8,128)(2,1)} %get-tuple-element.327, ...), kind=kOutput, calls=%fused_computation.3.clone.1 | convolution fusion | flops 561971200 | bytes 40386564 | tf_op jit(solution)/shard_map/while/body/eval_jaxpr/rjhd,rkhd->rhjk/dot_general | solution.py:81
  279.5 16.8 %fusion.62 = f32[128,2,256]{2,1,0:T(2,128)S(1)} fusion(f32[128,2,128,256]{3,2,1,0:T(8,128)} %get-tuple-element.292, f32[128,2,256]{2,1,0:T(2,128)S(1)} %fusion.61, f32[2,256,128]{1,2,0:T(8,128)S(1)} %constant_dynamic-slice_fusion.4, pred[128,128]{1,0:T(8,128)(4,1)S(1)} %constant_dynamic-slice_fusion.5), kind=kLoop, calls=%fused_computation.5.clone.1 | loop fusion | flops 41877504 | bytes 34357248 | tf_op jit(solution)/shard_map/while/body/eval_jaxpr/reduce_sum | solution.py:88
  296.9 15.0 %fusion.64 = f32[128,2,256,32]{2,3,1,0:T(8,128)S(1)} fusion(f32[128,2,256,32]{2,3,1,0:T(8,128)S(1)} %copy-done.2, f32[128,2,256]{2,1,0:T(2,128)S(1)} %get-tuple-element.294, pred[]{:T(512)S(6)} %compare.4, f32[128,2,128,256]{3,2,1,0:T(8,128)} %get-tuple-element.292, f32[128,2,256]{2,1,0:T(2,128)S(1)} %fusion.61, ...), kind=kOutput, calls=%fused_computation.9.clone.1 | convolution fusion | flops 585105408 | bytes 53231620 | tf_op jit(solution)/shard_map/while/body/eval_jaxpr/rhjk,rkhd->rhjd/dot_general | solution.py:89
  311.9 3.2 copy-done.3
  315.3 16.2 %fusion.60 = (f32[128,2,256]{2,1,0:T(2,128)S(1)}, f32[128,2,128,256]{3,2,1,0:T(8,128)}) fusion(f32[2,256,128]{1,2,0:T(8,128)S(1)} %constant_dynamic-slice_fusion.4, pred[128,128]{1,0:T(8,128)(4,1)S(1)} %constant_dynamic-slice_fusion.5, bf16[128,256,2,32]{1,3,2,0:T(8,128)(2,1)} %get-tuple-element.327, ...), kind=kOutput, calls=%fused_computation.3.clone.1 | convolution fusion | flops 561971200 | bytes 40386564 | tf_op jit(solution)/shard_map/while/body/eval_jaxpr/rjhd,rkhd->rhjk/dot_general | solution.py:81
  331.7 16.8 %fusion.62 = f32[128,2,256]{2,1,0:T(2,128)S(1)} fusion(f32[128,2,128,256]{3,2,1,0:T(8,128)} %get-tuple-element.292, f32[128,2,256]{2,1,0:T(2,128)S(1)} %fusion.61, f32[2,256,128]{1,2,0:T(8,128)S(1)} %constant_dynamic-slice_fusion.4, pred[128,128]{1,0:T(8,128)(4,1)S(1)} %constant_dynamic-slice_fusion.5), kind=kLoop, calls=%fused_computation.5.clone.1 | loop fusion | flops 41877504 | bytes 34357248 | tf_op jit(solution)/shard_map/while/body/eval_jaxpr/reduce_sum | solution.py:88
  349.0 15.0 %fusion.64 = f32[128,2,256,32]{2,3,1,0:T(8,128)S(1)} fusion(f32[128,2,256,32]{2,3,1,0:T(8,128)S(1)} %copy-done.2, f32[128,2,256]{2,1,0:T(2,128)S(1)} %get-tuple-element.294, pred[]{:T(512)S(6)} %compare.4, f32[128,2,128,256]{3,2,1,0:T(8,128)} %get-tuple-element.292, f32[128,2,256]{2,1,0:T(2,128)S(1)} %fusion.61, ...), kind=kOutput, calls=%fused_computation.9.clone.1 | convolution fusion | flops 585105408 | bytes 53231620 | tf_op jit(solution)/shard_map/while/body/eval_jaxpr/rhjk,rkhd->rhjd/dot_general | solution.py:89
  367.4 16.2 %fusion.60 = (f32[128,2,256]{2,1,0:T(2,128)S(1)}, f32[128,2,128,256]{3,2,1,0:T(8,128)}) fusion(f32[2,256,128]{1,2,0:T(8,128)S(1)} %constant_dynamic-slice_fusion.4, pred[128,128]{1,0:T(8,128)(4,1)S(1)} %constant_dynamic-slice_fusion.5, bf16[128,256,2,32]{1,3,2,0:T(8,128)(2,1)} %get-tuple-element.327, ...), kind=kOutput, calls=%fused_computation.3.clone.1 | convolution fusion | flops 561971200 | bytes 40386564 | tf_op jit(solution)/shard_map/while/body/eval_jaxpr/rjhd,rkhd->rhjk/dot_general | solution.py:81
  383.8 16.8 %fusion.62 = f32[128,2,256]{2,1,0:T(2,128)S(1)} fusion(f32[128,2,128,256]{3,2,1,0:T(8,128)} %get-tuple-element.292, f32[128,2,256]{2,1,0:T(2,128)S(1)} %fusion.61, f32[2,256,128]{1,2,0:T(8,128)S(1)} %constant_dynamic-slice_fusion.4, pred[128,128]{1,0:T(8,128)(4,1)S(1)} %constant_dynamic-slice_fusion.5), kind=kLoop, calls=%fused_computation.5.clone.1 | loop fusion | flops 41877504 | bytes 34357248 | tf_op jit(solution)/shard_map/while/body/eval_jaxpr/reduce_sum | solution.py:88
  401.2 15.0 %fusion.64 = f32[128,2,256,32]{2,3,1,0:T(8,128)S(1)} fusion(f32[128,2,256,32]{2,3,1,0:T(8,128)S(1)} %copy-done.2, f32[128,2,256]{2,1,0:T(2,128)S(1)} %get-tuple-element.294, pred[]{:T(512)S(6)} %compare.4, f32[128,2,128,256]{3,2,1,0:T(8,128)} %get-tuple-element.292, f32[128,2,256]{2,1,0:T(2,128)S(1)} %fusion.61, ...), kind=kOutput, calls=%fused_computation.9.clone.1 | convolution fusion | flops 585105408 | bytes 53231620 | tf_op jit(solution)/shard_map/while/body/eval_jaxpr/rhjk,rkhd->rhjd/dot_general | solution.py:89
  419.6 16.2 %fusion.60 = (f32[128,2,256]{2,1,0:T(2,128)S(1)}, f32[128,2,128,256]{3,2,1,0:T(8,128)}) fusion(f32[2,256,128]{1,2,0:T(8,128)S(1)} %constant_dynamic-slice_fusion.4, pred[128,128]{1,0:T(8,128)(4,1)S(1)} %constant_dynamic-slice_fusion.5, bf16[128,256,2,32]{1,3,2,0:T(8,128)(2,1)} %get-tuple-element.327, ...), kind=kOutput, calls=%fused_computation.3.clone.1 | convolution fusion | flops 561971200 | bytes 40386564 | tf_op jit(solution)/shard_map/while/body/eval_jaxpr/rjhd,rkhd->rhjk/dot_general | solution.py:81
  436.0 16.8 %fusion.62 = f32[128,2,256]{2,1,0:T(2,128)S(1)} fusion(f32[128,2,128,256]{3,2,1,0:T(8,128)} %get-tuple-element.292, f32[128,2,256]{2,1,0:T(2,128)S(1)} %fusion.61, f32[2,256,128]{1,2,0:T(8,128)S(1)} %constant_dynamic-slice_fusion.4, pred[128,128]{1,0:T(8,128)(4,1)S(1)} %constant_dynamic-slice_fusion.5), kind=kLoop, calls=%fused_computation.5.clone.1 | loop fusion | flops 41877504 | bytes 34357248 | tf_op jit(solution)/shard_map/while/body/eval_jaxpr/reduce_sum | solution.py:88
  453.4 15.0 %fusion.64 = f32[128,2,256,32]{2,3,1,0:T(8,128)S(1)} fusion(f32[128,2,256,32]{2,3,1,0:T(8,128)S(1)} %copy-done.2, f32[128,2,256]{2,1,0:T(2,128)S(1)} %get-tuple-element.294, pred[]{:T(512)S(6)} %compare.4, f32[128,2,128,256]{3,2,1,0:T(8,128)} %get-tuple-element.292, f32[128,2,256]{2,1,0:T(2,128)S(1)} %fusion.61, ...), kind=kOutput, calls=%fused_computation.9.clone.1 | convolution fusion | flops 585105408 | bytes 53231620 | tf_op jit(solution)/shard_map/while/body/eval_jaxpr/rhjk,rkhd->rhjd/dot_general | solution.py:89
  471.8 5.0 divide_convert_fusion
  477.6 4.6 convolution_convert_fusion.2
  482.2 16.4 %reduce-scatter.2.cloned.1.call-done = bf16[128,128,128]{2,1,0:T(8,128)(2,1)} async-done(((bf16[128,256,128]{2,1,0:T(8,128)(2,1)}), bf16[128,128,128]{2,1,0:T(8,128)(2,1)}) %reduce-scatter.2.cloned.1.call-update) | async-done | bytes 4194320 | tf_op jit(solution)/shard_map/reduce_scatter | solution.py:104
  (83 shorter events, 24.4 us)
Async XLA Ops:
  6.5 470.3 %copy-start = (bf16[128,128]{1,0:T(8,128)(2,1)S(1)}, bf16[128,128]{1,0:T(8,128)(2,1)}, u32[]{:S(2)}) copy-start(bf16[128,128]{1,0:T(8,128)(2,1)} %param.21) | copy-start | bytes 98308
  6.5 16.8 %copy-start.9 = (f32[128]{0:T(128)S(1)}, f32[128]{0:T(128)}, u32[]{:S(2)}) copy-start(f32[128]{0:T(128)} %param.15) | copy-start | bytes 1540
  6.5 151.0 %all-gather.3.cloned.1.call-start = ((), (), s32[]{:S(2)}) async-start(), calls=%async_computation.2 | async-start | bytes 12582912 | tf_op jit(solution)/shard_map/all_gather | solution.py:70
  6.5 16.8 %slice-start = ((s8[8388608]{0:T(1024)(128)(4,1)}), s8[4194304]{0:T(1024)(128)(4,1)S(1)}, s32[]{:S(2)}) async-start(s8[8388608]{0:T(1024)(128)(4,1)} %bitcast.82), calls=%async_computation.5 | async-start | bytes 8388608
  12.4 10.9 %slice-start.1 = ((s8[8388608]{0:T(1024)(128)(4,1)}), s8[4194304]{0:T(1024)(128)(4,1)S(1)}, s32[]{:S(2)}) async-start(s8[8388608]{0:T(1024)(128)(4,1)} %bitcast.82), calls=%async_computation.6 | async-start | bytes 8388608
  23.3 13.2 %copy-start.5 = (bf16[128,64]{0,1:T(8,128)(2,1)S(1)}, bf16[128,64]{0,1:T(8,128)(2,1)}, u32[]{:S(2)}) copy-start(bf16[128,64]{0,1:T(8,128)(2,1)} %param.17) | copy-start | bytes 49156
  33.3 3.2 copy-start.1
  40.6 4.7 copy-start.6
  45.1 218.0 %all-gather.5.cloned.1.call-start = ((), (), s32[]{:S(2)}) async-start(), calls=%async_computation.3 | async-start | bytes 12582912 | tf_op jit(solution)/shard_map/all_gather | solution.py:71
  52.8 4.7 copy-start.10
  57.5 29.0 %copy-start.7 = (bf16[128,64]{0,1:T(8,128)(2,1)S(1)}, bf16[128,64]{0,1:T(8,128)(2,1)}, u32[]{:S(2)}) copy-start(bf16[128,64]{0,1:T(8,128)(2,1)} %param.16) | copy-start | bytes 49156
  64.3 30.6 %copy-start.11 = (bf16[128,64]{0,1:T(8,128)(2,1)S(1)}, bf16[128,64]{0,1:T(8,128)(2,1)}, u32[]{:S(2)}) copy-start(bf16[128,64]{0,1:T(8,128)(2,1)} %param.19) | copy-start | bytes 49156
  82.1 30.5 %all-to-all-start = ((bf16[2,512,256]{2,0,1:T(2,128)(2,1)}), bf16[2,512,256]{2,0,1:T(2,128)(2,1)S(1)}, u32[]{:S(2)}, u32[]{:S(2)}) async-start(bf16[2,512,256]{2,0,1:T(2,128)(2,1)} %all_gather.10), calls=%async_computation | async-start | bytes 1048576 | tf_op jit(solution)/shard_map/all_to_all | solution.py:62
  85.6 413.0 %reduce-scatter.2.cloned.1.call-start = ((), (), s32[]{:S(2)}) async-start(), calls=%async_computation.4 | async-start | bytes 12582912 | tf_op jit(solution)/shard_map/reduce_scatter | solution.py:104
  104.5 7.7 %copy-start.8 = (s32[128,4]{0,1:T(4,128)S(1)}, s32[128,4]{0,1:T(4,128)}, u32[]{:S(2)}) copy-start(s32[128,4]{0,1:T(4,128)} %param.14) | copy-start | bytes 6148
  279.5 17.4 %copy-start.2 = (f32[128,2,256,32]{2,3,1,0:T(8,128)S(1)}, f32[128,2,256,32]{2,3,1,0:T(8,128)}, u32[]{:S(2)}) copy-start(f32[128,2,256,32]{2,3,1,0:T(8,128)} %get-tuple-element.311) | copy-start | bytes 25165828 | tf_op jit(solution)/shard_map/while
  311.9 3.2 copy-start.3
  331.7 17.4 %copy-start.2 = (f32[128,2,256,32]{2,3,1,0:T(8,128)S(1)}, f32[128,2,256,32]{2,3,1,0:T(8,128)}, u32[]{:S(2)}) copy-start(f32[128,2,256,32]{2,3,1,0:T(8,128)} %get-tuple-element.311) | copy-start | bytes 25165828 | tf_op jit(solution)/shard_map/while
  364.1 3.2 copy-start.3
  383.8 17.4 %copy-start.2 = (f32[128,2,256,32]{2,3,1,0:T(8,128)S(1)}, f32[128,2,256,32]{2,3,1,0:T(8,128)}, u32[]{:S(2)}) copy-start(f32[128,2,256,32]{2,3,1,0:T(8,128)} %get-tuple-element.311) | copy-start | bytes 25165828 | tf_op jit(solution)/shard_map/while
  416.2 3.2 copy-start.3
  436.0 17.4 %copy-start.2 = (f32[128,2,256,32]{2,3,1,0:T(8,128)S(1)}, f32[128,2,256,32]{2,3,1,0:T(8,128)}, u32[]{:S(2)}) copy-start(f32[128,2,256,32]{2,3,1,0:T(8,128)} %get-tuple-element.311) | copy-start | bytes 25165828 | tf_op jit(solution)/shard_map/while
  468.4 3.2 copy-start.3
  471.8 5.8 %copy-start.4 = (f32[32768,64]{0,1:T(8,128)S(1)}, f32[32768,64]{0,1:T(8,128)}, u32[]{:S(2)}) copy-start(f32[32768,64]{0,1:T(8,128)} %fusion.22) | copy-start | bytes 25165828
Sparse Core Ops, SparseCore 0:
  45.2 112.2 all-gather.2
  159.1 103.9 all-gather.4
  482.3 16.2 reduce-scatter.1
where the time goes:
time: 506 us; the launch traced here: 505 us
  waiting for transfers between devices  166 us (33%)
  matrix products  164 us (32%)
  other arithmetic  102 us (20%)
  local copies, waits for them, and re-layouts  37.2 us (7%)
  blocking collectives  17.8 us (4%)
  between operations  14 us (3%)
    all_gather x1, waiting for transfers between devices, per_device(): piece_values = lax.all_gather(values_local, 'keys', axis=1, tiled=True)  106 us
    reduce_sum x4, other arithmetic, one_tile(): row_sum = row_sum * rescale + jnp.sum(weights, axis=-1)  67.2 us
    dot_general x4, matrix products, one_tile(): jnp.einsum('rjhd,rkhd->rhjk', queries, key_tile, preferred_element_type=j...  64.8 us
    dot_general x4, matrix products, one_tile(): jnp.einsum('rhjk,rkhd->rhjd', weights.astype(jnp.bfloat16), value_tile, p...  60.1 us
    all_gather x1, waiting for transfers between devices, per_device(): piece_keys = lax.all_gather(keys_local, 'keys', axis=1, tiled=True)  43.7 us
    all_gather x1, blocking collectives, per_device(): lax.all_gather(bias_local.astype(jnp.bfloat16), 'rows', axis=1, tiled=True)  17.8 us
    reduce_scatter x1, waiting for transfers between devices, per_device(): lax.psum_scatter(partial_out.astype(jnp.bfloat16), 'heads', scatter_dimen...  16.4 us
    unnamed x29, local copies, waits for them, and re-layouts  14 us
  transfers between devices with their start and end apart: 4, of which 3 were waited for; matrix products, arithmetic and copies ran while one was open for 9% of the time, Pallas kernels for 0%

commit v1 on v0

--- a/solution.py
+++ b/solution.py
@@ -67,8 +67,13 @@
         jnp.zeros((rows_dev, heads_dev, cols_dev), jnp.float32),
         jnp.zeros((rows_dev, heads_dev, cols_dev, HEAD_DIM), jnp.float32),
     )
-    piece_keys = lax.all_gather(keys_local, "keys", axis=1, tiled=True)
-    piece_values = lax.all_gather(values_local, "keys", axis=1, tiled=True)
+    piece_keys, piece_values = jnp.split(
+        lax.all_gather(
+            jnp.concatenate([keys_local, values_local], axis=0), "keys", axis=1, tiled=True
+        ),
+        [keys_local.shape[0]],
+        axis=0,
+    )
 
     def one_tile(tile_index, state):
         row_max, row_sum, weighted = state

time: 506 us -> 524 us (1.036)
  local copies, waits for them, and re-layouts: 37.2 us -> 46.2 us
  other arithmetic: 102 us -> 110 us
    split x0 -> x1, local copies, waits for them, and re-layouts: none -> 11.8 us  [per_device(): jnp.split(lax.all_gather(jnp.concatenate([keys_local, values_local], axis...]
    concatenate x0 -> x1, other arithmetic: none -> 7.41 us  [per_device(): jnp.concatenate([keys_local, values_local], axis=0)]
    all_gather x2 -> x1, waiting for transfers between devices: 149 us -> 151 us  [per_device(): lax.all_gather(jnp.concatenate([keys_local, values_local], axis=0), 'keys...]
  transfers between devices with their start and end apart: 4 -> 3, of which waited for: 3 -> 2; matrix products, arithmetic and copies ran while one was open for 9% -> 6% of each run, Pallas kernels for 0% -> 0%
where the time goes in v1:
time: 524 us; the launch traced here: 520 us
  waiting for transfers between devices  167 us (32%)
  matrix products  160 us (31%)
  other arithmetic  110 us (21%)
  local copies, waits for them, and re-layouts  46.2 us (9%)
  blocking collectives  18.1 us (3%)
  between operations  14.5 us (3%)
    all_gather x1, waiting for transfers between devices, per_device(): lax.all_gather(jnp.concatenate([keys_local, values_local], axis=0), 'keys...  151 us
    reduce_sum x4, other arithmetic, one_tile(): row_sum = row_sum * rescale + jnp.sum(weights, axis=-1)  67.2 us
    dot_general x4, matrix products, one_tile(): jnp.einsum('rjhd,rkhd->rhjk', queries, key_tile, preferred_element_type=j...  64.8 us
    dot_general x4, matrix products, one_tile(): jnp.einsum('rhjk,rkhd->rhjd', weights.astype(jnp.bfloat16), value_tile, p...  60.1 us
    all_gather x1, blocking collectives, per_device(): lax.all_gather(bias_local.astype(jnp.bfloat16), 'rows', axis=1, tiled=True)  18.1 us
    reduce_scatter x1, waiting for transfers between devices, per_device(): lax.psum_scatter(partial_out.astype(jnp.bfloat16), 'heads', scatter_dimen...  16.4 us
    while x20, local copies, waits for them, and re-layouts  12.9 us
    split x1, local copies, waits for them, and re-layouts, per_device(): jnp.split(lax.all_gather(jnp.concatenate([keys_local, values_local], axis...  11.8 us
  transfers between devices with their start and end apart: 3, of which 2 were waited for; matrix products, arithmetic and copies ran while one was open for 6% of the time, Pallas kernels for 0%

profile of v1, /device:TPU:0, one launch (start us, length us, event | category | flops | bytes accessed | tf_op | source)
XLA Modules:
  0.0 520.0 jit_solution(9727672341363336073)
XLA Ops:
  6.5 5.8 %convert_reduce_fusion = f32[128,256]{1,0:T(8,128)S(1)} fusion(bf16[128,256,128]{2,1,0:T(8,128)(2,1)} %param.12), kind=kLoop, calls=%fused_computation.33 | loop fusion | flops 8355840 | bytes 8519680 | tf_op jit(solution)/shard_map/reduce_sum | solution.py:13
  12.4 10.9 %fusion.25 = f32[128,256]{1,0:T(8,128)S(1)} fusion(bf16[128,256,128]{2,1,0:T(8,128)(2,1)} %param.12, f32[128,256]{1,0:T(8,128)S(1)} %broadcast_multiply_fusion), kind=kLoop, calls=%fused_computation.36 | loop fusion | flops 16744448 | bytes 8650752 | tf_op jit(solution)/shard_map/reduce_sum | solution.py:14
  23.3 10.4 %fusion.27 = bf16[128,256,128]{2,1,0:T(8,128)(2,1)S(1)} fusion(bf16[128,256,128]{2,1,0:T(8,128)(2,1)S(1)} %bitcast.83, f32[128]{0:T(128)S(1)} %copy-done.9, f32[128,256]{1,0:T(8,128)S(1)} %add_rsqrt_fusion, f32[128,256]{1,0:T(8,128)S(1)} %broadcast_multiply_fusion), kind=kLoop, calls=%fused_computation.38 | loop fusion | flops 20971520 | bytes 17039872 | tf_op jit(solution)/shard_map/convert_element_type | solution.py:34
  37.9 4.4 copy.20
  46.4 4.4 copy.21
  50.8 7.4 %pad_maximum_fusion = bf16[256,256,2,32]{1,3,2,0:T(8,128)(2,1)} fusion(bf16[128,256,2,32]{1,3,2,0:T(8,128)(2,1)} %copy.21, bf16[128,256,2,32]{1,3,2,0:T(8,128)(2,1)} %copy.20), kind=kLoop, calls=%fused_computation.41 | loop fusion | flops 4194304 | bytes 16777216 | tf_op jit(solution)/shard_map/concatenate | solution.py:72
  58.9 5.8 %fusion.30 = bf16[2,128,256]{2,0,1:T(2,128)(2,1)S(1)} fusion(bf16[128,256,128]{2,1,0:T(8,128)(2,1)} %copy-done.1, bf16[128,2]{0,1:T(2,128)(2,1)S(1)} %copy-done.10), kind=kOutput, calls=%fused_computation.45 | convolution fusion | flops 16842752 | bytes 8520192 | tf_op jit(solution)/shard_map/rkc,ch->hrk/dot_general | solution.py:54
  64.7 18.1 %all_gather.7 = bf16[2,512,256]{2,0,1:T(2,128)(2,1)} all-gather(bf16[2,128,256]{2,0,1:T(2,128)(2,1)S(1)} %fusion.30), channel_id=1, replica_groups=mesh['groups'=2,'rows'=4,'keys'=2,'heads'=2] {'rows'}, dimensions={1}, use_global_device_ids=true | all-gather | bytes 655360 | tf_op jit(solution)/shard_map/all_gather | solution.py:55
  82.9 3.5 all-to-all-start
  87.1 8.6 %fusion.21 = bf16[32768,64]{0,1:T(8,128)(2,1)} fusion(bf16[32768,128]{1,0:T(8,128)(2,1)} %bitcast.80, bf16[128,64]{0,1:T(8,128)(2,1)S(1)} %copy-done.7), kind=kOutput, calls=%fused_computation.28 | convolution fusion | flops 541065216 | bytes 12599296 | tf_op jit(solution)/shard_map/dot_general | solution.py:37
  95.7 9.8 %fusion.22 = f32[32768,64]{0,1:T(8,128)} fusion(bf16[32768,128]{1,0:T(8,128)(2,1)} %bitcast.81, bf16[128,64]{0,1:T(8,128)(2,1)S(1)} %copy-done.11), kind=kOutput, calls=%fused_computation.31 | convolution fusion | flops 543162368 | bytes 16793600 | tf_op jit(solution)/shard_map/dot_general | solution.py:51
  105.5 3.4 copy.30
  108.9 4.4 copy.23
  114.8 150.8 %all-gather.2.cloned.1.call-done = bf16[256,512,2,32]{1,3,2,0:T(8,128)(2,1)} async-done(((bf16[256,256,2,32]{1,3,2,0:T(8,128)(2,1)}), bf16[256,512,2,32]{1,3,2,0:T(8,128)(2,1)}) %all-gather.2.cloned.1.call-update) | async-done | bytes 16777232 | tf_op jit(solution)/shard_map/all_gather | solution.py:71
  265.6 11.8 %fusion.39 = (bf16[128,512,2,32]{1,3,2,0:T(8,128)(2,1)}, bf16[128,512,2,32]{1,3,2,0:T(8,128)(2,1)}) fusion(bf16[256,512,2,32]{1,3,2,0:T(8,128)(2,1)} %all-gather.2.cloned.1.call-done), kind=kLoop, calls=%fused_computation.62 | loop fusion | bytes 33554432 | tf_op jit(solution)/shard_map/split | solution.py:70
  277.4 208.6 %while.18 = (s32[]{:T(128)}, f32[128,2,256]{2,1,0:T(2,128)S(1)}, f32[128,2,256]{2,1,0:T(2,128)S(1)}, f32[128,2,256,32]{2,3,1,0:T(8,128)}, pred[128,512]{1,0:T(8,...) while((s32[]{:T(128)}, f32[128,2,256]{2,1,0:T(2,128)S(1)}, ...), condition=%wide.region_5.6_spmd.clone, body=%wide.region_2.5_spmd.clone.sunk | while | flops 1189412864 | bytes 198525168 | solution.py:102
  277.4 16.2 %fusion.61 = (f32[128,2,256]{2,1,0:T(2,128)S(1)}, f32[128,2,128,256]{3,2,1,0:T(8,128)}) fusion(f32[2,256,128]{1,2,0:T(8,128)S(1)} %constant_dynamic-slice_fusion.4, pred[128,128]{1,0:T(8,128)(4,1)S(1)} %constant_dynamic-slice_fusion.5, bf16[128,256,2,32]{1,3,2,0:T(8,128)(2,1)} %get-tuple-element.329, ...), kind=kOutput, calls=%fused_computation.3.clone.1 | convolution fusion | flops 561971200 | bytes 40386564 | tf_op jit(solution)/shard_map/while/body/eval_jaxpr/rjhd,rkhd->rhjk/dot_general | solution.py:86
  293.9 16.8 %fusion.63 = f32[128,2,256]{2,1,0:T(2,128)S(1)} fusion(f32[128,2,128,256]{3,2,1,0:T(8,128)} %get-tuple-element.294, f32[128,2,256]{2,1,0:T(2,128)S(1)} %fusion.62, f32[2,256,128]{1,2,0:T(8,128)S(1)} %constant_dynamic-slice_fusion.4, pred[128,128]{1,0:T(8,128)(4,1)S(1)} %constant_dynamic-slice_fusion.5), kind=kLoop, calls=%fused_computation.5.clone.1 | loop fusion | flops 41877504 | bytes 34357248 | tf_op jit(solution)/shard_map/while/body/eval_jaxpr/reduce_sum | solution.py:93
  311.2 15.0 %fusion.65 = f32[128,2,256,32]{2,3,1,0:T(8,128)S(1)} fusion(f32[128,2,256,32]{2,3,1,0:T(8,128)S(1)} %copy-done.2, f32[128,2,256]{2,1,0:T(2,128)S(1)} %get-tuple-element.296, pred[]{:T(512)S(6)} %compare.4, f32[128,2,128,256]{3,2,1,0:T(8,128)} %get-tuple-element.294, f32[128,2,256]{2,1,0:T(2,128)S(1)} %fusion.62, ...), kind=kOutput, calls=%fused_computation.9.clone.1 | convolution fusion | flops 585105408 | bytes 53231620 | tf_op jit(solution)/shard_map/while/body/eval_jaxpr/rhjk,rkhd->rhjd/dot_general | solution.py:94
  326.3 3.2 copy-done.3
  329.6 16.2 %fusion.61 = (f32[128,2,256]{2,1,0:T(2,128)S(1)}, f32[128,2,128,256]{3,2,1,0:T(8,128)}) fusion(f32[2,256,128]{1,2,0:T(8,128)S(1)} %constant_dynamic-slice_fusion.4, pred[128,128]{1,0:T(8,128)(4,1)S(1)} %constant_dynamic-slice_fusion.5, bf16[128,256,2,32]{1,3,2,0:T(8,128)(2,1)} %get-tuple-element.329, ...), kind=kOutput, calls=%fused_computation.3.clone.1 | convolution fusion | flops 561971200 | bytes 40386564 | tf_op jit(solution)/shard_map/while/body/eval_jaxpr/rjhd,rkhd->rhjk/dot_general | solution.py:86
  346.0 16.8 %fusion.63 = f32[128,2,256]{2,1,0:T(2,128)S(1)} fusion(f32[128,2,128,256]{3,2,1,0:T(8,128)} %get-tuple-element.294, f32[128,2,256]{2,1,0:T(2,128)S(1)} %fusion.62, f32[2,256,128]{1,2,0:T(8,128)S(1)} %constant_dynamic-slice_fusion.4, pred[128,128]{1,0:T(8,128)(4,1)S(1)} %constant_dynamic-slice_fusion.5), kind=kLoop, calls=%fused_computation.5.clone.1 | loop fusion | flops 41877504 | bytes 34357248 | tf_op jit(solution)/shard_map/while/body/eval_jaxpr/reduce_sum | solution.py:93
  363.4 15.0 %fusion.65 = f32[128,2,256,32]{2,3,1,0:T(8,128)S(1)} fusion(f32[128,2,256,32]{2,3,1,0:T(8,128)S(1)} %copy-done.2, f32[128,2,256]{2,1,0:T(2,128)S(1)} %get-tuple-element.296, pred[]{:T(512)S(6)} %compare.4, f32[128,2,128,256]{3,2,1,0:T(8,128)} %get-tuple-element.294, f32[128,2,256]{2,1,0:T(2,128)S(1)} %fusion.62, ...), kind=kOutput, calls=%fused_computation.9.clone.1 | convolution fusion | flops 585105408 | bytes 53231620 | tf_op jit(solution)/shard_map/while/body/eval_jaxpr/rhjk,rkhd->rhjd/dot_general | solution.py:94
  381.8 16.2 %fusion.61 = (f32[128,2,256]{2,1,0:T(2,128)S(1)}, f32[128,2,128,256]{3,2,1,0:T(8,128)}) fusion(f32[2,256,128]{1,2,0:T(8,128)S(1)} %constant_dynamic-slice_fusion.4, pred[128,128]{1,0:T(8,128)(4,1)S(1)} %constant_dynamic-slice_fusion.5, bf16[128,256,2,32]{1,3,2,0:T(8,128)(2,1)} %get-tuple-element.329, ...), kind=kOutput, calls=%fused_computation.3.clone.1 | convolution fusion | flops 561971200 | bytes 40386564 | tf_op jit(solution)/shard_map/while/body/eval_jaxpr/rjhd,rkhd->rhjk/dot_general | solution.py:86
  398.2 16.8 %fusion.63 = f32[128,2,256]{2,1,0:T(2,128)S(1)} fusion(f32[128,2,128,256]{3,2,1,0:T(8,128)} %get-tuple-element.294, f32[128,2,256]{2,1,0:T(2,128)S(1)} %fusion.62, f32[2,256,128]{1,2,0:T(8,128)S(1)} %constant_dynamic-slice_fusion.4, pred[128,128]{1,0:T(8,128)(4,1)S(1)} %constant_dynamic-slice_fusion.5), kind=kLoop, calls=%fused_computation.5.clone.1 | loop fusion | flops 41877504 | bytes 34357248 | tf_op jit(solution)/shard_map/while/body/eval_jaxpr/reduce_sum | solution.py:93
  415.6 15.0 %fusion.65 = f32[128,2,256,32]{2,3,1,0:T(8,128)S(1)} fusion(f32[128,2,256,32]{2,3,1,0:T(8,128)S(1)} %copy-done.2, f32[128,2,256]{2,1,0:T(2,128)S(1)} %get-tuple-element.296, pred[]{:T(512)S(6)} %compare.4, f32[128,2,128,256]{3,2,1,0:T(8,128)} %get-tuple-element.294, f32[128,2,256]{2,1,0:T(2,128)S(1)} %fusion.62, ...), kind=kOutput, calls=%fused_computation.9.clone.1 | convolution fusion | flops 585105408 | bytes 53231620 | tf_op jit(solution)/shard_map/while/body/eval_jaxpr/rhjk,rkhd->rhjd/dot_general | solution.py:94
  433.9 16.2 %fusion.61 = (f32[128,2,256]{2,1,0:T(2,128)S(1)}, f32[128,2,128,256]{3,2,1,0:T(8,128)}) fusion(f32[2,256,128]{1,2,0:T(8,128)S(1)} %constant_dynamic-slice_fusion.4, pred[128,128]{1,0:T(8,128)(4,1)S(1)} %constant_dynamic-slice_fusion.5, bf16[128,256,2,32]{1,3,2,0:T(8,128)(2,1)} %get-tuple-element.329, ...), kind=kOutput, calls=%fused_computation.3.clone.1 | convolution fusion | flops 561971200 | bytes 40386564 | tf_op jit(solution)/shard_map/while/body/eval_jaxpr/rjhd,rkhd->rhjk/dot_general | solution.py:86
  450.3 16.8 %fusion.63 = f32[128,2,256]{2,1,0:T(2,128)S(1)} fusion(f32[128,2,128,256]{3,2,1,0:T(8,128)} %get-tuple-element.294, f32[128,2,256]{2,1,0:T(2,128)S(1)} %fusion.62, f32[2,256,128]{1,2,0:T(8,128)S(1)} %constant_dynamic-slice_fusion.4, pred[128,128]{1,0:T(8,128)(4,1)S(1)} %constant_dynamic-slice_fusion.5), kind=kLoop, calls=%fused_computation.5.clone.1 | loop fusion | flops 41877504 | bytes 34357248 | tf_op jit(solution)/shard_map/while/body/eval_jaxpr/reduce_sum | solution.py:93
  467.7 15.0 %fusion.65 = f32[128,2,256,32]{2,3,1,0:T(8,128)S(1)} fusion(f32[128,2,256,32]{2,3,1,0:T(8,128)S(1)} %copy-done.2, f32[128,2,256]{2,1,0:T(2,128)S(1)} %get-tuple-element.296, pred[]{:T(512)S(6)} %compare.4, f32[128,2,128,256]{3,2,1,0:T(8,128)} %get-tuple-element.294, f32[128,2,256]{2,1,0:T(2,128)S(1)} %fusion.62, ...), kind=kOutput, calls=%fused_computation.9.clone.1 | convolution fusion | flops 585105408 | bytes 53231620 | tf_op jit(solution)/shard_map/while/body/eval_jaxpr/rhjk,rkhd->rhjd/dot_general | solution.py:94
  486.1 5.0 divide_convert_fusion
  491.9 4.6 convolution_convert_fusion.2
  496.5 16.4 %reduce-scatter.2.cloned.1.call-done = bf16[128,128,128]{2,1,0:T(8,128)(2,1)} async-done(((bf16[128,256,128]{2,1,0:T(8,128)(2,1)}), bf16[128,128,128]{2,1,0:T(8,128)(2,1)}) %reduce-scatter.2.cloned.1.call-update) | async-done | bytes 4194320 | tf_op jit(solution)/shard_map/reduce_scatter | solution.py:109
  (82 shorter events, 24.3 us)
Async XLA Ops:
  6.5 484.6 %copy-start = (bf16[128,128]{1,0:T(8,128)(2,1)S(1)}, bf16[128,128]{1,0:T(8,128)(2,1)}, u32[]{:S(2)}) copy-start(bf16[128,128]{1,0:T(8,128)(2,1)} %param.21) | copy-start | bytes 98308
  6.5 16.8 %copy-start.9 = (f32[128]{0:T(128)S(1)}, f32[128]{0:T(128)}, u32[]{:S(2)}) copy-start(f32[128]{0:T(128)} %param.15) | copy-start | bytes 1540
  6.5 259.0 %all-gather.2.cloned.1.call-start = ((), (), s32[]{:S(2)}) async-start(), calls=%async_computation.2 | async-start | bytes 25165824 | tf_op jit(solution)/shard_map/all_gather | solution.py:71
  6.5 16.8 %slice-start = ((s8[8388608]{0:T(1024)(128)(4,1)}), s8[4194304]{0:T(1024)(128)(4,1)S(1)}, s32[]{:S(2)}) async-start(s8[8388608]{0:T(1024)(128)(4,1)} %bitcast.82), calls=%async_computation.4 | async-start | bytes 8388608
  12.4 10.9 %slice-start.1 = ((s8[8388608]{0:T(1024)(128)(4,1)}), s8[4194304]{0:T(1024)(128)(4,1)S(1)}, s32[]{:S(2)}) async-start(s8[8388608]{0:T(1024)(128)(4,1)} %bitcast.82), calls=%async_computation.5 | async-start | bytes 8388608
  23.3 10.4 %copy-start.5 = (bf16[128,64]{0,1:T(8,128)(2,1)S(1)}, bf16[128,64]{0,1:T(8,128)(2,1)}, u32[]{:S(2)}) copy-start(bf16[128,64]{0,1:T(8,128)(2,1)} %param.17) | copy-start | bytes 49156
  33.7 8.5 %copy-start.1 = (bf16[128,256,128]{2,1,0:T(8,128)(2,1)}, bf16[128,256,128]{2,1,0:T(8,128)(2,1)S(1)}, u32[]{:S(2)}) copy-start(bf16[128,256,128]{2,1,0:T(8,128)(2,1)S(1)} %fusion.27) | copy-start | bytes 25165828
  36.8 5.5 %copy-start.6 = (bf16[128,64]{0,1:T(8,128)(2,1)S(1)}, bf16[128,64]{0,1:T(8,128)(2,1)}, u32[]{:S(2)}) copy-start(bf16[128,64]{0,1:T(8,128)(2,1)} %param.18) | copy-start | bytes 49156
  58.2 0.7 copy-start.10
  58.9 28.2 %copy-start.7 = (bf16[128,64]{0,1:T(8,128)(2,1)S(1)}, bf16[128,64]{0,1:T(8,128)(2,1)}, u32[]{:S(2)}) copy-start(bf16[128,64]{0,1:T(8,128)(2,1)} %param.16) | copy-start | bytes 49156
  64.7 30.9 %copy-start.11 = (bf16[128,64]{0,1:T(8,128)(2,1)S(1)}, bf16[128,64]{0,1:T(8,128)(2,1)}, u32[]{:S(2)}) copy-start(bf16[128,64]{0,1:T(8,128)(2,1)} %param.19) | copy-start | bytes 49156
  82.9 30.8 %all-to-all-start = ((bf16[2,512,256]{2,0,1:T(2,128)(2,1)}), bf16[2,512,256]{2,0,1:T(2,128)(2,1)S(1)}, u32[]{:S(2)}, u32[]{:S(2)}) async-start(bf16[2,512,256]{2,0,1:T(2,128)(2,1)} %all_gather.7), calls=%async_computation | async-start | bytes 1048576 | tf_op jit(solution)/shard_map/all_to_all | solution.py:62
  86.4 426.6 %reduce-scatter.2.cloned.1.call-start = ((), (), s32[]{:S(2)}) async-start(), calls=%async_computation.3 | async-start | bytes 12582912 | tf_op jit(solution)/shard_map/reduce_scatter | solution.py:109
  105.5 7.8 %copy-start.8 = (s32[128,4]{0,1:T(4,128)S(1)}, s32[128,4]{0,1:T(4,128)}, u32[]{:S(2)}) copy-start(s32[128,4]{0,1:T(4,128)} %param.14) | copy-start | bytes 6148
  293.9 17.4 %copy-start.2 = (f32[128,2,256,32]{2,3,1,0:T(8,128)S(1)}, f32[128,2,256,32]{2,3,1,0:T(8,128)}, u32[]{:S(2)}) copy-start(f32[128,2,256,32]{2,3,1,0:T(8,128)} %get-tuple-element.313) | copy-start | bytes 25165828 | tf_op jit(solution)/shard_map/while
  326.3 3.2 copy-start.3
  346.0 17.4 %copy-start.2 = (f32[128,2,256,32]{2,3,1,0:T(8,128)S(1)}, f32[128,2,256,32]{2,3,1,0:T(8,128)}, u32[]{:S(2)}) copy-start(f32[128,2,256,32]{2,3,1,0:T(8,128)} %get-tuple-element.313) | copy-start | bytes 25165828 | tf_op jit(solution)/shard_map/while
  378.4 3.2 copy-start.3
  398.2 17.4 %copy-start.2 = (f32[128,2,256,32]{2,3,1,0:T(8,128)S(1)}, f32[128,2,256,32]{2,3,1,0:T(8,128)}, u32[]{:S(2)}) copy-start(f32[128,2,256,32]{2,3,1,0:T(8,128)} %get-tuple-element.313) | copy-start | bytes 25165828 | tf_op jit(solution)/shard_map/while
  430.6 3.2 copy-start.3
  450.3 17.4 %copy-start.2 = (f32[128,2,256,32]{2,3,1,0:T(8,128)S(1)}, f32[128,2,256,32]{2,3,1,0:T(8,128)}, u32[]{:S(2)}) copy-start(f32[128,2,256,32]{2,3,1,0:T(8,128)} %get-tuple-element.313) | copy-start | bytes 25165828 | tf_op jit(solution)/shard_map/while
  482.8 3.2 copy-start.3
  486.1 5.8 %copy-start.4 = (f32[32768,64]{0,1:T(8,128)S(1)}, f32[32768,64]{0,1:T(8,128)}, u32[]{:S(2)}) copy-start(f32[32768,64]{0,1:T(8,128)} %fusion.22) | copy-start | bytes 25165828
Sparse Core Ops, SparseCore 0:
  58.4 207.1 all-gather.1
  496.7 16.2 reduce-scatter.1
